TPU v7x, 32 devices: a whole 2x2x4 slice. The times are simulated.
32 devices in a mesh: blk: 16 (over z, y, x), rep: 2 (over core).
Axes of the slice: x: 2, y: 2, z: 4, core: 2. Of those that a mesh axis runs over, the one named last changes fastest.
Arguments:
- load_coef: bfloat16 [32, 2049, 256], P('blk', None, 'rep'), parts along dimension 2, may hold values from -0.29882812 to 0.29882812
- legendre: bfloat16 [32, 2049, 1024], P('blk'), may hold values from -0.125 to 0.125
- slab_orders: int32 [32], replicated, may hold values from 0 to 1023, as said below
- cycle_rows: int32 [1024], replicated, may hold values from 0 to 1023, each once
Outputs:
- potential: bfloat16 [1024, 128, 4096], P('blk', 'rep'), parts along dimension 1
- energy: float32 [128], P('rep'), parts along dimension 0
There are 2 independent parts, one for each index of `rep`. A program takes and returns all parts, laid end to end along the dimension named above; an argument that names none is the same for every part. Nothing has to cross between parts.
Inputs may be any that keep to these rules, and one draw needn't show every extreme that they name: `slab_orders`: values are distinct and below (2048) / 2. `cycle_rows`: each cycle appears once.
All inputs are finite; a program needn't handle non-finite values.
Results may differ from a plain program's by a relative error of at most 0.0055.
Values may be sent and summed in bfloat16 or wider, within the bound.
A program may use at most 192 MiB of HBM per device.

v0:
```python
import math

import jax
import jax.numpy as jnp
from jax import lax
from jax.sharding import PartitionSpec as P

NLON = 4096


def basis_rows(frequency):
    coarse_ids = jnp.arange(NLON // 64, dtype=jnp.int32) * 64
    fine_ids = jnp.arange(64, dtype=jnp.int32)
    scale = 2.0 * math.pi / NLON
    coarse_angles = (frequency[:, None] * coarse_ids[None, :] % NLON).astype(jnp.float32) * scale
    fine_angles = (frequency[:, None] * fine_ids[None, :] % NLON).astype(jnp.float32) * scale
    cos_coarse = jnp.cos(coarse_angles)[:, :, None]
    sin_coarse = jnp.sin(coarse_angles)[:, :, None]
    cos_fine = jnp.cos(fine_angles)[:, None, :]
    sin_fine = jnp.sin(fine_angles)[:, None, :]
    cosine = (cos_coarse * cos_fine - sin_coarse * sin_fine).reshape(frequency.shape[0], NLON)
    sine = (sin_coarse * cos_fine + cos_coarse * sin_fine).reshape(frequency.shape[0], NLON)
    factor = jnp.where(frequency == 0, 1.0, 2.0).astype(jnp.float32)[:, None]
    return ((factor * cosine).astype(jnp.bfloat16), (-factor * sine).astype(jnp.bfloat16))


def fourier(received, low_orders, degree):
    cos_lower, sin_lower = basis_rows(low_orders)
    cos_upper, sin_upper = basis_rows(degree - low_orders)
    fourier_basis = jnp.stack([cos_lower, sin_lower, cos_upper, sin_upper], axis=1)
    return jnp.einsum("rnsf,nsk->rfk", received, fourier_basis, preferred_element_type=jnp.float32)


def shards(load_coef, legendre, slab_orders, cycle_rows):
    blocks = lax.axis_size("blk")
    position = lax.axis_index("blk")
    pair_count = load_coef.shape[0]
    slab_rows = load_coef.shape[1]
    fields = load_coef.shape[2] // 2
    lat_count = legendre.shape[2]
    cycle_count = lat_count // blocks
    degree = slab_rows - 2
    my_orders = lax.dynamic_slice_in_dim(slab_orders, position * pair_count, pair_count)
    row_ids = jnp.arange(slab_rows, dtype=jnp.int32)
    spectra = []
    for pair_index in range(pair_count):
        in_lower = (row_ids < slab_rows - 1 - my_orders[pair_index])[:, None]
        pair_coef = load_coef[pair_index]
        nothing = jnp.zeros_like(pair_coef)
        stacked = jnp.concatenate(
            [jnp.where(in_lower, pair_coef, nothing), jnp.where(in_lower, nothing, pair_coef)],
            axis=1,
        )
        spectra.append(
            lax.dot_general(
                legendre[pair_index],
                stacked,
                (((0,), (0,)), ((), ())),
                preferred_element_type=jnp.float32,
            ).astype(jnp.bfloat16)
        )
    spectra = jnp.stack(spectra, axis=1).reshape(lat_count, pair_count, 4, fields)
    spectra = jnp.take(spectra, cycle_rows, axis=0)
    all_orders = slab_orders.reshape(blocks, pair_count)
    cycle_grid = jnp.zeros((cycle_count, fields, NLON), jnp.float32)
    for pair_index in range(pair_count):
        cycle_grid = cycle_grid + fourier(
            lax.all_to_all(
                spectra[:, pair_index : pair_index + 1],
                "blk",
                split_axis=0,
                concat_axis=1,
                tiled=True,
            ),
            low_orders=all_orders[:, pair_index],
            degree=degree,
        )
    partial_energy = jnp.sum(cycle_grid * cycle_grid, axis=(0, 2))
    summed = lax.psum(partial_energy, "blk")
    energy = summed / (lat_count * NLON)
    return (cycle_grid.astype(jnp.bfloat16), energy)


def solution(mesh):
    in_specs = (P("blk", None, "rep"), P("blk", None, None), P(), P())
    out_specs = (P("blk", "rep", None), P("rep"))
    return jax.shard_map(shards, mesh=mesh, in_specs=in_specs, out_specs=out_specs, check_vma=False)
```

profile of v0, /device:TPU:0, one launch (start us, length us, event | category | flops | bytes accessed | tf_op | source)
XLA Modules:
  0.0 187.0 jit_solution(15199914749275640568)
XLA Ops:
  0.6 0.7 compare_and_fusion
  2.0 0.7 dynamic_slice.3
  4.7 3.6 %fusion.90 = (bf16[1,2049,128]{2,0,1:T(2,128)(2,1)S(1)}, bf16[1,2049,128]{2,0,1:T(2,128)(2,1)S(1)}) fusion(bf16[2,2049,128]{2,0,1:T(2,128)(2,1)} %param.4), kind=kLoop, calls=%fused_computation.175 | loop fusion | bytes 2098176 | tf_op jit(solution)/shard_map/slice | solution.py:48
  8.3 17.4 %fusion.88 = (bf16[1,2049,1024]{2,0,1:T(2,128)(2,1)}, bf16[1,2049,1024]{2,0,1:T(2,128)(2,1)S(1)}) fusion(bf16[2,2049,1024]{2,0,1:T(2,128)(2,1)} %param.5), kind=kLoop, calls=%fused_computation.173 | loop fusion | bytes 16785408 | tf_op jit(solution)/shard_map/slice | solution.py:56
  25.7 1.9 %broadcast_select_fusion.2 = (bf16[2049,128]{1,0:T(8,128)(2,1)S(1)}, bf16[2049,128]{1,0:T(8,128)(2,1)S(1)}, bf16[2049,128]{1,0:T(8,128)(2,1)S(1)}, bf16[2049,128]{1,0:T(8,128)(2,1)S(1)}) fusion(pred[2049]{0:T(1024)(128)(4,1)S(1)} %iota_compare_fusion, bf16[1,2049,128]{2,0,1:T(2,128)(2,1)S(1)} %get-tuple-element.25, ...), kind=kLoop, calls=%fused_computation.25 | loop fusion | flops 1049088 | bytes 3151362 | tf_op jit(solution)/shard_map/jit(_where)/select_n | solution.py:51
  27.6 1.5 fusion.3
  29.2 0.7 copy.12
  29.9 4.9 %fusion.2 = bf16[256,1024]{1,0:T(8,128)(2,1)S(1)} fusion(bf16[1,2049,1024]{2,0,1:T(2,128)(2,1)} %get-tuple-element.16, bf16[2049,128]{1,0:T(8,128)(2,1)S(1)} %get-tuple-element.71, bf16[2049,128]{1,0:T(8,128)(2,1)S(1)} %get-tuple-element.72), kind=kOutput, calls=%fused_computation.9 | convolution fusion | flops 1076626432 | bytes 5769728 | tf_op jit(solution)/shard_map/dot_general | solution.py:55
  34.8 0.7 copy.11
  35.5 3.1 %pad_maximum_fusion = bf16[1024,2,4,64]{3,2,1,0:T(4,128)(2,1)} fusion(bf16[1024,1,4,64]{3,2,1,0:T(4,128)(2,1)S(1)} %copy.12, bf16[1024,1,4,64]{3,2,1,0:T(4,128)(2,1)S(1)} %copy.11), kind=kLoop, calls=%fused_computation.7 | loop fusion | flops 524288 | bytes 2097152 | tf_op jit(solution)/shard_map/stack | solution.py:62
  38.6 5.8 %gather_fusion = bf16[1024,2,4,64]{3,2,1,0:T(4,128)(2,1)S(1)} fusion(bf16[1024,2,4,64]{3,2,1,0:T(4,128)(2,1)} %pad_maximum_fusion, s32[1024]{0:T(1024)S(1)} %fusion.83), kind=kCustom, calls=%fused_computation | custom fusion | bytes 2101248 | tf_op jit(solution)/shard_map/jit(_take)/gather | solution.py:63
  44.4 3.8 %broadcast_select_fusion = bf16[1024,2,4,64]{3,2,1,0:T(4,128)(2,1)S(1)} fusion(bf16[1024,2,4,64]{3,2,1,0:T(4,128)(2,1)S(1)} %gather_fusion, pred[1024]{0:T(1024)(128)(4,1)S(1)} %compare_and_fusion), kind=kLoop, calls=%fused_computation.8 | loop fusion | flops 524288 | bytes 2098176 | tf_op jit(solution)/shard_map/jit(_take)/select_n | solution.py:63
  48.3 0.7 fusion.89
  49.0 1.5 reshape.1147
  50.5 8.3 %all-to-all-start = ((bf16[16,2,8192]{2,1,0:T(2,128)(2,1)}), bf16[16,2,8192]{2,1,0:T(2,128)(2,1)S(1)}, u32[]{:S(2)}, u32[]{:S(2)}) async-start(bf16[16,2,8192]{2,1,0:T(2,128)(2,1)} %reshape.1147), calls=%async_computation | async-start | bytes 1048576 | tf_op jit(solution)/shard_map/all_to_all | solution.py:68
  59.6 1.4 multiply_subtract_fusion
  61.0 1.9 %sub.99 = f32[16,1,4096]{2,0,1:T(8,128)} reshape(f32[16,64,64]{2,1,0:T(8,128)} %get-tuple-element.28) | data formatting | bytes 524288 | tf_op jit(solution)/shard_map/sub | solution.py:21
  62.9 0.9 add.180
  63.8 0.9 add.176
  64.9 1.4 multiply_subtract_fusion.2
  66.3 1.9 %sub.93 = f32[16,1,4096]{2,0,1:T(8,128)} reshape(f32[16,64,64]{2,1,0:T(8,128)} %get-tuple-element.32) | data formatting | bytes 524288 | tf_op jit(solution)/shard_map/sub | solution.py:21
  68.2 0.9 add.172
  69.6 1.0 multiply_convert_fusion.1
  70.7 1.7 multiply_convert_fusion
  72.3 1.7 multiply_convert_fusion.2
  74.0 0.7 multiply_convert_fusion.3
  74.7 1.0 multiply_convert_fusion.5
  76.1 1.5 reshape.1149
  77.8 6.9 %all-to-all-start.1 = ((bf16[16,2,8192]{2,1,0:T(2,128)(2,1)}), bf16[16,2,8192]{2,1,0:T(2,128)(2,1)S(1)}, u32[]{:S(2)}, u32[]{:S(2)}) async-start(bf16[16,2,8192]{2,1,0:T(2,128)(2,1)} %reshape.1149), calls=%async_computation.1 | async-start | bytes 1048576 | tf_op jit(solution)/shard_map/all_to_all | solution.py:68
  85.4 23.2 %fusion.11 = f32[64,64,4096,1]{2,1,3,0:T(8,128)} fusion(bf16[16,64,1,4,64]{4,3,1,0,2:T(4,128)(2,1)S(1)} %bitcast.61, bf16[16,1,4096]{2,0,1:T(8,128)(2,1)S(1)} %multiply_convert_fusion.4, bf16[16,1,4096]{2,0,1:T(8,128)(2,1)S(1)} %multiply_convert_fusion.5, bf16[16,1,4096]{2,0,1:T(8,128)(2,1)S(1)} %multiply_convert_fusion.6, ...), kind=kOutput, calls=%fused_computation.18 | convolution fusion | flops 2148270080 | bytes 68157440 | tf_op jit(solution)/shard_map/rnsf,nsk->rfk/dot_general | solution.py:31
  109.3 35.2 %multiply_reduce_fusion = (f32[64]{0:T(128)S(1)}, bf16[64,64,4096]{2,1,0:T(8,128)(2,1)}) fusion(bf16[16,1,4096]{2,0,1:T(8,128)(2,1)S(1)} %copy-done.1, bf16[16,1,4096]{2,0,1:T(8,128)(2,1)S(1)} %multiply_convert_fusion.1, bf16[16,1,4096]{2,0,1:T(8,128)(2,1)S(1)} %copy-done.2, bf16[16,1,4096]{2,0,1:T(8,128)(2,1)S(1)} %copy-done.3, ...), kind=kOutput, calls=%fused_computation.2 | convolution fusion | flops 2215378944 | bytes 101712128 | tf_op jit(solution)/shard_map/rnsf,nsk->rfk/dot_general | solution.py:31
  144.4 42.1 %psum.7 = f32[64]{0:T(128)S(1)} all-reduce(f32[64]{0:T(128)S(1)} %get-tuple-element.14), channel_id=1, replica_groups=mesh['blk'=16,'rep'=2] {'blk'}, use_global_device_ids=true, to_apply=%region_1.2 | all-reduce | flops 64 | bytes 512 | tf_op jit(solution)/shard_map/psum | solution.py:79
  (32 shorter events, 5.0 us)
Async XLA Ops:
  49.0 9.9 %copy-start.4 = (s32[32]{0:T(128)S(1)}, s32[32]{0:T(128)}, u32[]{:S(2)}) copy-start(s32[32]{0:T(128)} %param.6) | copy-start | bytes 388
  50.5 27.2 %all-to-all-start = ((bf16[16,2,8192]{2,1,0:T(2,128)(2,1)}), bf16[16,2,8192]{2,1,0:T(2,128)(2,1)S(1)}, u32[]{:S(2)}, u32[]{:S(2)}) async-start(bf16[16,2,8192]{2,1,0:T(2,128)(2,1)} %reshape.1147), calls=%async_computation | async-start | bytes 1048576 | tf_op jit(solution)/shard_map/all_to_all | solution.py:68
  69.1 6.7 %copy-start = (f32[16,1,4096]{2,0,1:T(8,128)S(1)}, f32[16,1,4096]{2,0,1:T(8,128)}, u32[]{:S(2)}) copy-start(f32[16,1,4096]{2,0,1:T(8,128)} %add.172) | copy-start | bytes 786436
  77.8 30.8 %all-to-all-start.1 = ((bf16[16,2,8192]{2,1,0:T(2,128)(2,1)}), bf16[16,2,8192]{2,1,0:T(2,128)(2,1)S(1)}, u32[]{:S(2)}, u32[]{:S(2)}) async-start(bf16[16,2,8192]{2,1,0:T(2,128)(2,1)} %reshape.1149), calls=%async_computation.1 | async-start | bytes 1048576 | tf_op jit(solution)/shard_map/all_to_all | solution.py:68
  85.3 23.9 %copy-start.1 = (bf16[16,1,4096]{2,0,1:T(8,128)(2,1)S(1)}, bf16[16,1,4096]{2,0,1:T(8,128)(2,1)}, u32[]{:S(2)}) copy-start(bf16[16,1,4096]{2,0,1:T(8,128)(2,1)} %multiply_convert_fusion) | copy-start | bytes 393220
  85.3 23.9 %copy-start.2 = (bf16[16,1,4096]{2,0,1:T(8,128)(2,1)S(1)}, bf16[16,1,4096]{2,0,1:T(8,128)(2,1)}, u32[]{:S(2)}) copy-start(bf16[16,1,4096]{2,0,1:T(8,128)(2,1)} %multiply_convert_fusion.2) | copy-start | bytes 393220
  85.4 23.9 %copy-start.3 = (bf16[16,1,4096]{2,0,1:T(8,128)(2,1)S(1)}, bf16[16,1,4096]{2,0,1:T(8,128)(2,1)}, u32[]{:S(2)}) copy-start(bf16[16,1,4096]{2,0,1:T(8,128)(2,1)} %multiply_convert_fusion.3) | copy-start | bytes 393220
where the time goes:
time: 188 us; the launch traced here: 187 us
  matrix products  64.8 us (34%)
  blocking collectives  42.1 us (22%)
  local copies, waits for them, and re-layouts  41.8 us (22%)
  other arithmetic  20.9 us (11%)
  starting transfers between devices  15.3 us (8%)
  between operations  2.17 us (1%)
    dot_general x2, matrix products, fourier(): jnp.einsum('rnsf,nsk->rfk', received, fourier_basis, preferred_element_ty...  58.4 us
    psum x1, blocking collectives, shards(): summed = lax.psum(partial_energy, 'blk')  42.1 us
    slice x1, local copies, waits for them, and re-layouts, shards(): legendre[pair_index]  17.4 us
    all_to_all x2, starting transfers between devices, shards(): lax.all_to_all(spectra[:, pair_index:pair_index + 1], 'blk', split_axis=0...  15.3 us
    dot_general x2, matrix products, shards(): lax.dot_general(legendre[pair_index], stacked, (((0,), (0,)), ((), ())),...  6.43 us
    gather x1, local copies, waits for them, and re-layouts, shards(): spectra = jnp.take(spectra, cycle_rows, axis=0)  5.81 us
    unnamed x14, local copies, waits for them, and re-layouts  4.35 us
    sub x4, local copies, waits for them, and re-layouts, basis_rows(): cos_coarse * cos_fine - sin_coarse * sin_fine  4.24 us
  transfers between devices with their start and end apart: 2, of which 0 were waited for; matrix products, arithmetic and copies ran while one was open for 23% of the time, Pallas kernels for 0%

commit v1 on v0

v1 whole, which is shorter than its diff:
```python
import functools
import math

import jax
import jax.numpy as jnp
from jax import lax
from jax.experimental import pallas as pl
from jax.experimental.pallas import tpu as pltpu
from jax.sharding import PartitionSpec as P

NLON = 4096
LANES = 128
MESH = pl.DeviceIdType.MESH


def spectra_kernel(pairs, orders_ref, table_ref, coef_ref, rows_ref, send_ref, energy_ref, masked, spectra, staging):
    step = pl.program_id(0)
    packed_rows, block = table_ref.shape
    slab_rows = packed_rows // pairs
    streams = masked.shape[0] // (2 * pairs)

    @pl.when(step == 0)
    def _():
        flipped = jnp.transpose(coef_ref[...].astype(jnp.float32))
        packed_id = lax.broadcasted_iota(jnp.int32, flipped.shape, 1)
        row_id = packed_id // pairs
        pair_id = packed_id % pairs
        for pair in range(pairs):
            lower = row_id < slab_rows - 1 - orders_ref[pair]
            mine = pair_id == pair
            for half in range(2):
                keep = mine & (lower if half == 0 else ~lower)
                start = (2 * pair + half) * streams
                masked[start : start + streams, :] = jnp.where(keep, flipped, 0.0).astype(jnp.bfloat16)

    product = jnp.dot(masked[:, :packed_rows], table_ref[...], preferred_element_type=jnp.float32)
    spectra[:, pl.ds(pl.multiple_of(step * block, block), block)] = product.astype(jnp.bfloat16)

    @pl.when(step == pl.num_programs(0) - 1)
    def _():
        lat_count = spectra.shape[1]
        fields = streams // 2
        groups = lat_count // 2
        kinds = 4 * pairs
        chunk = min(256, groups)
        total = jnp.zeros((1, kinds * fields), jnp.float32)
        for start in range(0, groups, chunk):
            sorted_rows = []
            for parity in range(2):
                wanted = rows_ref[parity * groups + start : parity * groups + start + chunk, :]
                cycle_id = lax.broadcasted_iota(jnp.int32, (chunk, lat_count), 1)
                chosen = (wanted == cycle_id).astype(jnp.float32).astype(jnp.bfloat16)
                rows = lax.dot_general(chosen, spectra[...], (((1,), (1,)), ((), ())), preferred_element_type=jnp.float32)
                total = total + jnp.sum(rows * rows, axis=0, keepdims=True)
                sorted_rows.append(rows)
            for kind in range(kinds):
                lanes = slice(kind * fields, (kind + 1) * fields)
                staging[pl.ds(start * kinds + kind, chunk, stride=kinds), :] = jnp.concatenate([sorted_rows[0][:, lanes], sorted_rows[1][:, lanes]], axis=1)
        energy = jnp.zeros((1, streams), jnp.float32)
        lane_id = lax.broadcasted_iota(jnp.int32, (1, streams), 1)
        for index in range(2 * pairs):
            part = total[:, index * streams : (index + 1) * streams]
            if index % 2 == 0:
                constant = orders_ref[index // 2] == 0
                weight = jnp.where(constant, jnp.where(lane_id < fields, 1.0, 0.0), 2.0)
            else:
                weight = 2.0
            energy = energy + weight * part
        energy_ref[...] = jnp.broadcast_to(energy, energy_ref.shape)
        send_ref[...] = staging[...].reshape(send_ref.shape).astype(jnp.bfloat16)


def exchange_kernel(n, degree, send_ref, energy_ref, orders_ref, recv_ref, basis_ref, total_ref, energies, send_sem, recv_sem, esend_sem, erecv_sem, own_sem):
    me = lax.axis_index("blk")
    barrier = pltpu.get_barrier_semaphore()

    def signal(s, carry):
        pl.semaphore_signal(barrier, inc=1, device_id={"blk": lax.rem(me + s, n)}, device_id_type=MESH)
        return carry

    lax.fori_loop(1, n, signal, 0)
    pl.semaphore_wait(barrier, n - 1)

    def block_copy(s):
        peer = lax.rem(me + s, n)
        return pltpu.make_async_remote_copy(
            src_ref=send_ref.at[peer], dst_ref=recv_ref.at[me], send_sem=send_sem.at[s], recv_sem=recv_sem.at[s],
            device_id={"blk": peer}, device_id_type=MESH)

    def energy_copy(s):
        peer = lax.rem(me + s, n)
        return pltpu.make_async_remote_copy(
            src_ref=energy_ref, dst_ref=energies.at[s], send_sem=esend_sem.at[s], recv_sem=erecv_sem.at[s],
            device_id={"blk": peer}, device_id_type=MESH)

    def start(s, carry):
        energy_copy(s).start()
        block_copy(s).start()
        return carry

    lax.fori_loop(1, n, start, 0)
    own = pltpu.make_async_copy(send_ref.at[me], recv_ref.at[me], own_sem)
    own.start()

    rows = basis_ref.shape[0]
    row_id = lax.broadcasted_iota(jnp.int32, (rows, LANES), 0)
    lane_id = lax.broadcasted_iota(jnp.int32, (rows, LANES), 1)
    low = jnp.broadcast_to(orders_ref[...], (rows, LANES))
    order = jnp.where((row_id & 2) == 0, low, degree - low)
    scale = 2.0 * math.pi / NLON
    turn = (order * (LANES * lane_id) + (row_id & 1) * (NLON // 4)) & (NLON - 1)
    fine = (order * lane_id) & (NLON - 1)
    factor = jnp.where(order == 0, 1.0, 2.0)
    coarse_angle = turn.astype(jnp.float32) * scale
    fine_angle = fine.astype(jnp.float32) * scale
    cos_coarse, sin_coarse = factor * jnp.cos(coarse_angle), factor * jnp.sin(coarse_angle)
    cos_fine, sin_fine = jnp.cos(fine_angle), jnp.sin(fine_angle)
    for tile in range(NLON // LANES):
        values = cos_coarse[:, tile : tile + 1] * cos_fine - sin_coarse[:, tile : tile + 1] * sin_fine
        basis_ref[:, tile * LANES : (tile + 1) * LANES] = values.astype(jnp.bfloat16)

    def finish_energy(s, total):
        energy_copy(s).wait()
        return total + energies[s]

    total_ref[...] = lax.fori_loop(1, n, finish_energy, energy_ref[...])

    def finish(s, carry):
        block_copy(s).wait()
        return carry

    lax.fori_loop(1, n, finish, 0)
    own.wait()


def wave_kernel(recv_ref, basis_ref, out_ref, held):
    groups = recv_ref.shape[1]
    depth = basis_ref.shape[0]
    for group in range(groups):
        values = recv_ref[:, group, :, :].astype(jnp.float32).reshape(depth, LANES)
        held[group * LANES : (group + 1) * LANES, :] = jnp.transpose(values).astype(jnp.bfloat16)
    width = 512

    @pl.loop(0, NLON // width)
    def _(tile):
        columns = pl.ds(pl.multiple_of(tile * width, width), width)
        wave = jnp.dot(held[...], basis_ref[:, columns], preferred_element_type=jnp.float32)
        out_ref[:, :, columns] = wave.astype(jnp.bfloat16).reshape(out_ref.shape[0], out_ref.shape[1], width)


def shards(load_coef, legendre, slab_orders, cycle_rows):
    n = lax.axis_size("blk")
    position = lax.axis_index("blk")
    pairs, slab_rows, streams = load_coef.shape
    fields = streams // 2
    lat_count = legendre.shape[2]
    cycle_count = lat_count // n
    per_tile = LANES // fields
    groups = cycle_count // per_tile
    kinds = 4 * pairs
    degree = slab_rows - 2
    packed_rows = slab_rows * pairs
    padded = -(-packed_rows // LANES) * LANES
    table = jnp.transpose(legendre, (1, 0, 2)).reshape(packed_rows, lat_count)
    coef = jnp.transpose(load_coef, (1, 0, 2)).reshape(packed_rows, streams)
    coef = jnp.pad(coef, ((0, padded - packed_rows), (0, 0)))
    my_orders = lax.dynamic_slice_in_dim(slab_orders, position * pairs, pairs)
    wanted = jnp.transpose(cycle_rows.reshape(lat_count // 2, 2)).reshape(lat_count, 1)
    steps = 4
    block = lat_count // steps
    send, energy = pl.pallas_call(
        functools.partial(spectra_kernel, pairs),
        grid_spec=pltpu.PrefetchScalarGridSpec(
            num_scalar_prefetch=1,
            grid=(steps,),
            in_specs=[
                pl.BlockSpec((packed_rows, block), lambda s, o: (0, s)),
                pl.BlockSpec((padded, streams), lambda s, o: (0, 0), pipeline_mode=pl.Buffered(1)),
                pl.BlockSpec((lat_count, 1), lambda s, o: (0, 0), pipeline_mode=pl.Buffered(1)),
            ],
            out_specs=[
                pl.BlockSpec((n, groups, kinds, LANES), lambda s, o: (0, 0, 0, 0)),
                pl.BlockSpec((8, streams), lambda s, o: (0, 0)),
            ],
            scratch_shapes=[
                pltpu.VMEM((2 * pairs * streams, padded), jnp.bfloat16),
                pltpu.VMEM((2 * pairs * streams, lat_count), jnp.bfloat16),
                pltpu.VMEM((n * groups * kinds, LANES), jnp.float32),
            ],
        ),
        out_shape=[
            jax.ShapeDtypeStruct((n, groups, kinds, LANES), jnp.bfloat16),
            jax.ShapeDtypeStruct((8, streams), jnp.float32),
        ],
        compiler_params=pltpu.CompilerParams(dimension_semantics=("arbitrary",)),
    )(my_orders, table, coef, wanted)
    order_rows = jnp.repeat(slab_orders, 4).reshape(n * kinds, 1)
    recv, basis, total = pl.pallas_call(
        functools.partial(exchange_kernel, n, degree),
        out_shape=[
            jax.ShapeDtypeStruct((n, groups, kinds, LANES), jnp.bfloat16),
            jax.ShapeDtypeStruct((n * kinds, NLON), jnp.bfloat16),
            jax.ShapeDtypeStruct((8, streams), jnp.float32),
        ],
        in_specs=[
            pl.BlockSpec(memory_space=pl.ANY),
            pl.BlockSpec(memory_space=pltpu.VMEM),
            pl.BlockSpec(memory_space=pltpu.VMEM),
        ],
        out_specs=[
            pl.BlockSpec(memory_space=pl.ANY),
            pl.BlockSpec(memory_space=pltpu.VMEM),
            pl.BlockSpec(memory_space=pltpu.VMEM),
        ],
        scratch_shapes=[
            pltpu.VMEM((n, 8, streams), jnp.float32),
            pltpu.SemaphoreType.DMA((n,)),
            pltpu.SemaphoreType.DMA((n,)),
            pltpu.SemaphoreType.DMA((n,)),
            pltpu.SemaphoreType.DMA((n,)),
            pltpu.SemaphoreType.DMA,
        ],
        compiler_params=pltpu.CompilerParams(collective_id=0, has_side_effects=True),
    )(send, energy, order_rows)
    step_groups = min(4, groups)
    potential = pl.pallas_call(
        wave_kernel,
        grid=(groups // step_groups,),
        out_shape=jax.ShapeDtypeStruct((cycle_count, fields, NLON), jnp.bfloat16),
        in_specs=[
            pl.BlockSpec((n, step_groups, kinds, LANES), lambda s: (0, s, 0, 0)),
            pl.BlockSpec((n * kinds, NLON), lambda s: (0, 0), pipeline_mode=pl.Buffered(1)),
        ],
        out_specs=pl.BlockSpec((step_groups * per_tile, fields, NLON), lambda s: (s, 0, 0)),
        scratch_shapes=[pltpu.VMEM((step_groups * LANES, n * kinds), jnp.bfloat16)],
        compiler_params=pltpu.CompilerParams(dimension_semantics=("arbitrary",)),
    )(recv, basis)
    energy = (total[0, :fields] + total[0, fields:]) / lat_count
    return potential, energy


def solution(mesh):
    in_specs = (P("blk", None, "rep"), P("blk", None, None), P(), P())
    out_specs = (P("blk", "rep", None), P("rep"))
    return jax.shard_map(shards, mesh=mesh, in_specs=in_specs, out_specs=out_specs, check_vma=False)
```

time: 188 us -> 96.4 us (0.51)
  the two profiles are of different devices: /device:TPU:0 before, /device:TPU:15 now
where the time goes in v1:
time: 96.4 us; the launch traced here: 95.6 us
  Pallas kernels  67.2 us (70%)
  local copies, waits for them, and re-layouts  26.4 us (27%)
  other arithmetic  1.33 us (1%)
    pallas_call x1, Pallas kernels, shards(): pl.pallas_call(functools.partial(exchange_kernel, n, degree), out_shape=[...  32.8 us
    pallas_call x1, Pallas kernels, shards(): pl.pallas_call(wave_kernel, grid=(groups // step_groups,), out_shape=jax....  22.7 us
    reshape x1, local copies, waits for them, and re-layouts, shards(): table = jnp.transpose(legendre, (1, 0, 2)).reshape(packed_rows, lat_count)  17.9 us
    pallas_call x1, Pallas kernels, shards(): pl.pallas_call(functools.partial(spectra_kernel, pairs), grid_spec=pltpu....  11.6 us
    reshape x1, local copies, waits for them, and re-layouts, shards(): coef = jnp.transpose(load_coef, (1, 0, 2)).reshape(packed_rows, streams)  2.68 us

profile of v1, /device:TPU:15, one launch (start us, length us, event | category | flops | bytes accessed | tf_op | source)
XLA Modules:
  0.0 95.6 jit_solution(13547062134241518644)
XLA Ops:
  0.6 1.2 %dynamic_slice.3.orders_ref = s32[2]{0:T(128)} dynamic-slice(s32[32]{0:T(128)} %param.6, s32[]{:T(128)S(6)} %select_n.3), dynamic_slice_sizes={2} | dynamic-slice | bytes 20 | tf_op jit(solution)/shard_map/dynamic_slice | solution.py:167
  1.9 0.7 broadcast_in_dim.3
  2.6 0.7 reshape_reshape.4.orders_ref
  3.3 0.9 reshape.21
  4.2 0.1 copy.7
  4.3 1.1 %copy.11 = s32[1,1024]{0,1:T(8,128)} copy(s32[1,1024]{1,0:T(1,128)S(1)} %bitcast.14) | data formatting | bytes 8192
  5.4 2.7 %reshape.20 = bf16[4098,128]{1,0:T(8,128)(2,1)S(1)} reshape(bf16[2049,2,128]{2,1,0:T(2,128)(2,1)} %bitcast.11) | data formatting | bytes 2098176 | tf_op jit(solution)/shard_map/reshape | solution.py:165
  8.1 1.1 %pad.4.coef_ref = bf16[4224,128]{1,0:T(8,128)(2,1)} pad(bf16[4098,128]{1,0:T(8,128)(2,1)S(1)} %reshape.20, bf16[]{:T(256)} %constant.15.clone.1), padding=0_126x0_0 | pad | bytes 2130434 | tf_op jit(solution)/shard_map/jit(_pad)/pad | solution.py:166
  9.2 17.9 %reshape.19.table_ref = bf16[4098,1024]{1,0:T(8,128)(2,1)} reshape(bf16[2049,2,1024]{2,1,0:T(2,128)(2,1)} %bitcast.9) | data formatting | bytes 16785408 | tf_op jit(solution)/shard_map/reshape | solution.py:164
  27.1 11.6 %shard_map.59 = (bf16[16,32,8,128]{3,2,1,0:T(8,128)(2,1)}, f32[8,128]{1,0:T(8,128)}) custom-call(s32[2]{0:T(128)} %dynamic_slice.3.orders_ref, bf16[4098,1024]{1,0:T(8,128)(2,1)} %reshape.19.table_ref, bf16[4224,128]{1,0:T(8,128)(2,1)} %pad.4.coef_ref, s32[1024,1]{1,0:T(8,128)} %bitcast.10), custom_call_target="tpu_custom_call" | custom-call | tf_op jit(solution)/shard_map/pallas_call | solution.py:171
  38.7 32.8 %shard_map.60 = (bf16[16,32,8,128]{3,2,1,0:T(8,128)(2,1)}, bf16[128,4096]{1,0:T(8,128)(2,1)}, f32[8,128]{1,0:T(8,128)}) custom-call(bf16[16,32,8,128]{3,2,1,0:T(8,128)(2,1)} %get-tuple-element.7.send_ref, f32[8,128]{1,0:T(8,128)} %get-tuple-element.8.energy_ref, s32[128,1]{1,0:T(8,128)} %reshape_reshape.4.orders_ref), custom_call_target="tpu_custom_call" | custom-call | tf_op jit(solution)/shard_map/pallas_call | solution.py:198
  71.5 1.3 %multiply_bitcast_fusion = f32[64]{0:T(128)} fusion(f32[8,128]{1,0:T(8,128)} %get-tuple-element.11), kind=kLoop, calls=%fused_computation | loop fusion | flops 128 | bytes 768 | tf_op jit(solution)/shard_map/div | solution.py:238
  72.9 22.7 %shard_map.61 = bf16[64,64,4096]{2,1,0:T(8,128)(2,1)} custom-call(bf16[16,32,8,128]{3,2,1,0:T(8,128)(2,1)} %get-tuple-element.9.recv_ref, bf16[128,4096]{1,0:T(8,128)(2,1)} %get-tuple-element.10.basis_ref), custom_call_target="tpu_custom_call" | custom-call | tf_op jit(solution)/shard_map/pallas_call | solution.py:226
  (1 shorter events, 0.0 us)

commit v2 on v1

--- a/solution.py
+++ b/solution.py
@@ -13,55 +13,59 @@
 MESH = pl.DeviceIdType.MESH
 
 
-def spectra_kernel(pairs, orders_ref, table_ref, coef_ref, rows_ref, send_ref, energy_ref, masked, spectra, staging):
+def spectra_kernel(pairs, orders_ref, table_ref, coef_ref, rows_ref, send_ref, energy_ref, masked, spectra, sorted_rows, staging):
     step = pl.program_id(0)
-    packed_rows, block = table_ref.shape
-    slab_rows = packed_rows // pairs
+    first_pair = lax.axis_index("blk") * pairs
+    slab_rows, _, block = table_ref.shape
+    packed_rows = slab_rows * pairs
     streams = masked.shape[0] // (2 * pairs)
 
     @pl.when(step == 0)
     def _():
-        flipped = jnp.transpose(coef_ref[...].astype(jnp.float32))
+        packed = coef_ref[...].reshape(packed_rows, streams)
+        flipped = jnp.transpose(jnp.concatenate([packed, jnp.zeros((masked.shape[1] - packed_rows, streams), packed.dtype)], axis=0).astype(jnp.float32))
         packed_id = lax.broadcasted_iota(jnp.int32, flipped.shape, 1)
         row_id = packed_id // pairs
         pair_id = packed_id % pairs
         for pair in range(pairs):
-            lower = row_id < slab_rows - 1 - orders_ref[pair]
+            lower = row_id < slab_rows - 1 - orders_ref[first_pair + pair]
             mine = pair_id == pair
             for half in range(2):
                 keep = mine & (lower if half == 0 else ~lower)
                 start = (2 * pair + half) * streams
                 masked[start : start + streams, :] = jnp.where(keep, flipped, 0.0).astype(jnp.bfloat16)
 
-    product = jnp.dot(masked[:, :packed_rows], table_ref[...], preferred_element_type=jnp.float32)
+    product = jnp.dot(masked[:, :packed_rows], table_ref[...].reshape(packed_rows, block), preferred_element_type=jnp.float32)
     spectra[:, pl.ds(pl.multiple_of(step * block, block), block)] = product.astype(jnp.bfloat16)
 
     @pl.when(step == pl.num_programs(0) - 1)
     def _():
         lat_count = spectra.shape[1]
         fields = streams // 2
-        groups = lat_count // 2
         kinds = 4 * pairs
-        chunk = min(256, groups)
+        columns = jnp.transpose(rows_ref[...].astype(jnp.float32))
+        cycle_id = lax.broadcasted_iota(jnp.int32, (LANES, lat_count), 1).astype(jnp.float32)
         total = jnp.zeros((1, kinds * fields), jnp.float32)
-        for start in range(0, groups, chunk):
-            sorted_rows = []
-            for parity in range(2):
-                wanted = rows_ref[parity * groups + start : parity * groups + start + chunk, :]
-                cycle_id = lax.broadcasted_iota(jnp.int32, (chunk, lat_count), 1)
-                chosen = (wanted == cycle_id).astype(jnp.float32).astype(jnp.bfloat16)
-                rows = lax.dot_general(chosen, spectra[...], (((1,), (1,)), ((), ())), preferred_element_type=jnp.float32)
-                total = total + jnp.sum(rows * rows, axis=0, keepdims=True)
-                sorted_rows.append(rows)
-            for kind in range(kinds):
-                lanes = slice(kind * fields, (kind + 1) * fields)
-                staging[pl.ds(start * kinds + kind, chunk, stride=kinds), :] = jnp.concatenate([sorted_rows[0][:, lanes], sorted_rows[1][:, lanes]], axis=1)
+        half = LANES // 2
+        for part in range(lat_count // LANES):
+            chosen = (columns[:, part : part + 1] == cycle_id).astype(jnp.float32).astype(jnp.bfloat16)
+            rows = lax.dot_general(chosen, spectra[...], (((1,), (1,)), ((), ())), preferred_element_type=jnp.float32)
+            total = total + jnp.sum(rows * rows, axis=0, keepdims=True)
+            for order in range(2 * pairs):
+                sorted_rows[part, order] = rows[:, order * streams : (order + 1) * streams]
+                even = sorted_rows[part, order, pl.ds(0, half, stride=2), :]
+                odd = sorted_rows[part, order, pl.ds(1, half, stride=2), :]
+                real = jnp.concatenate([even[:, :fields], odd[:, :fields]], axis=1)
+                imag = jnp.concatenate([even[:, fields:], odd[:, fields:]], axis=1)
+                first = part * half * kinds + 2 * order
+                staging[pl.ds(first, half, stride=kinds), :] = real
+                staging[pl.ds(first + 1, half, stride=kinds), :] = imag
         energy = jnp.zeros((1, streams), jnp.float32)
         lane_id = lax.broadcasted_iota(jnp.int32, (1, streams), 1)
         for index in range(2 * pairs):
             part = total[:, index * streams : (index + 1) * streams]
             if index % 2 == 0:
-                constant = orders_ref[index // 2] == 0
+                constant = orders_ref[first_pair + index // 2] == 0
                 weight = jnp.where(constant, jnp.where(lane_id < fields, 1.0, 0.0), 2.0)
             else:
                 weight = 2.0
@@ -105,7 +109,11 @@
     rows = basis_ref.shape[0]
     row_id = lax.broadcasted_iota(jnp.int32, (rows, LANES), 0)
     lane_id = lax.broadcasted_iota(jnp.int32, (rows, LANES), 1)
-    low = jnp.broadcast_to(orders_ref[...], (rows, LANES))
+    width = orders_ref.shape[1]
+    pair_row = lax.broadcasted_iota(jnp.int32, (rows, width), 0) // 4
+    pair_lane = lax.broadcasted_iota(jnp.int32, (rows, width), 1)
+    spread = jnp.where(pair_row == pair_lane, orders_ref[...].astype(jnp.float32), 0.0)
+    low = jnp.broadcast_to(jnp.sum(spread, axis=1, keepdims=True), (rows, LANES)).astype(jnp.int32)
     order = jnp.where((row_id & 2) == 0, low, degree - low)
     scale = 2.0 * math.pi / NLON
     turn = (order * (LANES * lane_id) + (row_id & 1) * (NLON // 4)) & (NLON - 1)
@@ -133,24 +141,28 @@
     own.wait()
 
 
-def wave_kernel(recv_ref, basis_ref, out_ref, held):
+def wave_kernel(scale, recv_ref, basis_ref, total_ref, out_ref, energy_ref, held):
     groups = recv_ref.shape[1]
     depth = basis_ref.shape[0]
+    fields = out_ref.shape[1]
     for group in range(groups):
         values = recv_ref[:, group, :, :].astype(jnp.float32).reshape(depth, LANES)
         held[group * LANES : (group + 1) * LANES, :] = jnp.transpose(values).astype(jnp.bfloat16)
-    width = 512
+    width = min(NLON, NLON * LANES // depth)
 
     @pl.loop(0, NLON // width)
     def _(tile):
         columns = pl.ds(pl.multiple_of(tile * width, width), width)
-        wave = jnp.dot(held[...], basis_ref[:, columns], preferred_element_type=jnp.float32)
-        out_ref[:, :, columns] = wave.astype(jnp.bfloat16).reshape(out_ref.shape[0], out_ref.shape[1], width)
+        for cycle in range(out_ref.shape[0]):
+            rows = held[cycle * fields : (cycle + 1) * fields, :]
+            wave = jnp.dot(rows, basis_ref[:, columns], preferred_element_type=jnp.float32)
+            out_ref[cycle, :, columns] = wave.astype(jnp.bfloat16)
+
+    energy_ref[...] = (total_ref[0:1, :fields] + total_ref[0:1, fields:]) * scale
 
 
 def shards(load_coef, legendre, slab_orders, cycle_rows):
     n = lax.axis_size("blk")
-    position = lax.axis_index("blk")
     pairs, slab_rows, streams = load_coef.shape
     fields = streams // 2
     lat_count = legendre.shape[2]
@@ -161,11 +173,8 @@
     degree = slab_rows - 2
     packed_rows = slab_rows * pairs
     padded = -(-packed_rows // LANES) * LANES
-    table = jnp.transpose(legendre, (1, 0, 2)).reshape(packed_rows, lat_count)
-    coef = jnp.transpose(load_coef, (1, 0, 2)).reshape(packed_rows, streams)
-    coef = jnp.pad(coef, ((0, padded - packed_rows), (0, 0)))
-    my_orders = lax.dynamic_slice_in_dim(slab_orders, position * pairs, pairs)
-    wanted = jnp.transpose(cycle_rows.reshape(lat_count // 2, 2)).reshape(lat_count, 1)
+    table = jnp.transpose(legendre, (1, 0, 2))
+    coef = jnp.transpose(load_coef, (1, 0, 2))
     steps = 4
     block = lat_count // steps
     send, energy = pl.pallas_call(
@@ -174,9 +183,9 @@
             num_scalar_prefetch=1,
             grid=(steps,),
             in_specs=[
-                pl.BlockSpec((packed_rows, block), lambda s, o: (0, s)),
-                pl.BlockSpec((padded, streams), lambda s, o: (0, 0), pipeline_mode=pl.Buffered(1)),
-                pl.BlockSpec((lat_count, 1), lambda s, o: (0, 0), pipeline_mode=pl.Buffered(1)),
+                pl.BlockSpec((slab_rows, pairs, block), lambda s, o: (0, 0, s)),
+                pl.BlockSpec((slab_rows, pairs, streams), lambda s, o: (0, 0, 0), pipeline_mode=pl.Buffered(1)),
+                pl.BlockSpec((lat_count // LANES, LANES), lambda s, o: (0, 0), pipeline_mode=pl.Buffered(1)),
             ],
             out_specs=[
                 pl.BlockSpec((n, groups, kinds, LANES), lambda s, o: (0, 0, 0, 0)),
@@ -185,6 +194,7 @@
             scratch_shapes=[
                 pltpu.VMEM((2 * pairs * streams, padded), jnp.bfloat16),
                 pltpu.VMEM((2 * pairs * streams, lat_count), jnp.bfloat16),
+                pltpu.VMEM((lat_count // LANES, 2 * pairs, LANES, streams), jnp.float32),
                 pltpu.VMEM((n * groups * kinds, LANES), jnp.float32),
             ],
         ),
@@ -193,8 +203,7 @@
             jax.ShapeDtypeStruct((8, streams), jnp.float32),
         ],
         compiler_params=pltpu.CompilerParams(dimension_semantics=("arbitrary",)),
-    )(my_orders, table, coef, wanted)
-    order_rows = jnp.repeat(slab_orders, 4).reshape(n * kinds, 1)
+    )(slab_orders, table, coef, cycle_rows.reshape(lat_count // LANES, LANES))
     recv, basis, total = pl.pallas_call(
         functools.partial(exchange_kernel, n, degree),
         out_shape=[
@@ -221,22 +230,28 @@
             pltpu.SemaphoreType.DMA,
         ],
         compiler_params=pltpu.CompilerParams(collective_id=0, has_side_effects=True),
-    )(send, energy, order_rows)
+    )(send, energy, slab_orders.reshape(1, n * pairs))
     step_groups = min(4, groups)
-    potential = pl.pallas_call(
-        wave_kernel,
+    potential, mean_square = pl.pallas_call(
+        functools.partial(wave_kernel, 1.0 / lat_count),
         grid=(groups // step_groups,),
-        out_shape=jax.ShapeDtypeStruct((cycle_count, fields, NLON), jnp.bfloat16),
+        out_shape=[
+            jax.ShapeDtypeStruct((cycle_count, fields, NLON), jnp.bfloat16),
+            jax.ShapeDtypeStruct((1, fields), jnp.float32),
+        ],
         in_specs=[
             pl.BlockSpec((n, step_groups, kinds, LANES), lambda s: (0, s, 0, 0)),
             pl.BlockSpec((n * kinds, NLON), lambda s: (0, 0), pipeline_mode=pl.Buffered(1)),
-        ],
-        out_specs=pl.BlockSpec((step_groups * per_tile, fields, NLON), lambda s: (s, 0, 0)),
+            pl.BlockSpec((8, streams), lambda s: (0, 0), pipeline_mode=pl.Buffered(1)),
+        ],
+        out_specs=[
+            pl.BlockSpec((step_groups * per_tile, fields, NLON), lambda s: (s, 0, 0)),
+            pl.BlockSpec((1, fields), lambda s: (0, 0)),
+        ],
         scratch_shapes=[pltpu.VMEM((step_groups * LANES, n * kinds), jnp.bfloat16)],
         compiler_params=pltpu.CompilerParams(dimension_semantics=("arbitrary",)),
-    )(recv, basis)
-    energy = (total[0, :fields] + total[0, fields:]) / lat_count
-    return potential, energy
+    )(recv, basis, total)
+    return potential, mean_square.reshape(fields)
 
 
 def solution(mesh):

time: 96.4 us -> 63.2 us (0.66)
  local copies, waits for them, and re-layouts: 26.4 us -> 0 us
  Pallas kernels: 67.2 us -> 62.3 us
  other arithmetic: 1.33 us -> 0 us
    reshape x3 -> x0, local copies, waits for them, and re-layouts: 21.5 us -> none  [the longest x1 17.9 us: shards(): table = jnp.transpose(legendre, (1, 0, 2)).reshape(packed_rows, lat_count)]
    pallas_call x1, Pallas kernels: 22.7 us -> 16 us  [shards(): pl.pallas_call(functools.partial(wave_kernel, 1.0 / lat_count), grid=(gro...]
    pallas_call x1, Pallas kernels: 11.6 us -> 13.6 us  [shards(): pl.pallas_call(functools.partial(spectra_kernel, pairs), grid_spec=pltpu....]
    div x1 -> x0, other arithmetic: 1.33 us -> none  [shards(): energy = (total[0, :fields] + total[0, fields:]) / lat_count]
    dynamic_slice x1 -> x0, local copies, waits for them, and re-layouts: 1.24 us -> none  [shards(): my_orders = lax.dynamic_slice_in_dim(slab_orders, position * pairs, pairs)]
    pad x1 -> x0, local copies, waits for them, and re-layouts: 1.11 us -> none  [shards(): coef = jnp.pad(coef, ((0, padded - packed_rows), (0, 0)))]
    unnamed x2 -> x0, local copies, waits for them, and re-layouts: 1.07 us -> none
where the time goes in v2:
time: 63.2 us; the launch traced here: 63 us
  Pallas kernels  62.3 us (99%)
  between operations  0.64 us (1%)
    pallas_call x1, Pallas kernels, shards(): pl.pallas_call(functools.partial(exchange_kernel, n, degree), out_shape=[...  32.7 us
    pallas_call x1, Pallas kernels, shards(): pl.pallas_call(functools.partial(wave_kernel, 1.0 / lat_count), grid=(gro...  16 us
    pallas_call x1, Pallas kernels, shards(): pl.pallas_call(functools.partial(spectra_kernel, pairs), grid_spec=pltpu....  13.6 us

profile of v2, /device:TPU:15, one launch (start us, length us, event | category | flops | bytes accessed | tf_op | source)
XLA Modules:
  0.0 63.0 jit_solution(12573377871072436199)
XLA Ops:
  0.6 13.6 %shard_map.59 = (bf16[16,32,8,128]{3,2,1,0:T(8,128)(2,1)}, f32[8,128]{1,0:T(8,128)}) custom-call(s32[32]{0:T(128)} %orders_ref.1, bf16[2049,2,1024]{2,1,0:T(2,128)(2,1)} %bitcast.5, bf16[2049,2,128]{2,1,0:T(2,128)(2,1)} %bitcast.6, s32[8,128]{1,0:T(8,128)} %bitcast.7), custom_call_target="tpu_custom_call" | custom-call | tf_op jit(solution)/shard_map/pallas_call | solution.py:180
  14.3 32.7 %shard_map.60 = (bf16[16,32,8,128]{3,2,1,0:T(8,128)(2,1)}, bf16[128,4096]{1,0:T(8,128)(2,1)}, f32[8,128]{1,0:T(8,128)}) custom-call(bf16[16,32,8,128]{3,2,1,0:T(8,128)(2,1)} %get-tuple-element.9.send_ref, f32[8,128]{1,0:T(8,128)} %get-tuple-element.10.energy_ref, s32[1,32]{1,0:T(1,128)} %bitcast.8), custom_call_target="tpu_custom_call" | custom-call | tf_op jit(solution)/shard_map/pallas_call | solution.py:207
  46.9 16.0 %shard_map.61 = (bf16[64,64,4096]{2,1,0:T(8,128)(2,1)}, f32[1,64]{1,0:T(1,128)}) custom-call(bf16[16,32,8,128]{3,2,1,0:T(8,128)(2,1)} %get-tuple-element.11.recv_ref, bf16[128,4096]{1,0:T(8,128)(2,1)} %get-tuple-element.12.basis_ref, f32[8,128]{1,0:T(8,128)} %get-tuple-element.13.total_ref), custom_call_target="tpu_custom_call" | custom-call | tf_op jit(solution)/shard_map/pallas_call | solution.py:235

commit v3 on v2

--- a/solution.py
+++ b/solution.py
@@ -47,19 +47,25 @@
         cycle_id = lax.broadcasted_iota(jnp.int32, (LANES, lat_count), 1).astype(jnp.float32)
         total = jnp.zeros((1, kinds * fields), jnp.float32)
         half = LANES // 2
-        for part in range(lat_count // LANES):
-            chosen = (columns[:, part : part + 1] == cycle_id).astype(jnp.float32).astype(jnp.bfloat16)
+        batch = min(4, lat_count // LANES)
+        for first_part in range(0, lat_count // LANES, batch):
+            chosen = jnp.concatenate(
+                [(columns[:, first_part + i : first_part + i + 1] == cycle_id).astype(jnp.float32).astype(jnp.bfloat16) for i in range(batch)],
+                axis=0,
+            )
             rows = lax.dot_general(chosen, spectra[...], (((1,), (1,)), ((), ())), preferred_element_type=jnp.float32)
             total = total + jnp.sum(rows * rows, axis=0, keepdims=True)
-            for order in range(2 * pairs):
-                sorted_rows[part, order] = rows[:, order * streams : (order + 1) * streams]
-                even = sorted_rows[part, order, pl.ds(0, half, stride=2), :]
-                odd = sorted_rows[part, order, pl.ds(1, half, stride=2), :]
-                real = jnp.concatenate([even[:, :fields], odd[:, :fields]], axis=1)
-                imag = jnp.concatenate([even[:, fields:], odd[:, fields:]], axis=1)
-                first = part * half * kinds + 2 * order
-                staging[pl.ds(first, half, stride=kinds), :] = real
-                staging[pl.ds(first + 1, half, stride=kinds), :] = imag
+            for part in range(first_part, first_part + batch):
+                offset = (part - first_part) * LANES
+                for order in range(2 * pairs):
+                    sorted_rows[part, order] = rows[offset : offset + LANES, order * streams : (order + 1) * streams]
+                    even = sorted_rows[part, order, pl.ds(0, half, stride=2), :]
+                    odd = sorted_rows[part, order, pl.ds(1, half, stride=2), :]
+                    real = jnp.concatenate([even[:, :fields], odd[:, :fields]], axis=1)
+                    imag = jnp.concatenate([even[:, fields:], odd[:, fields:]], axis=1)
+                    first = part * half * kinds + 2 * order
+                    staging[pl.ds(first, half, stride=kinds), :] = real
+                    staging[pl.ds(first + 1, half, stride=kinds), :] = imag
         energy = jnp.zeros((1, streams), jnp.float32)
         lane_id = lax.broadcasted_iota(jnp.int32, (1, streams), 1)
         for index in range(2 * pairs):

time: 63.2 us -> 61.8 us (0.978)
  Pallas kernels: 62.3 us -> 60.9 us
    pallas_call x1, Pallas kernels: 13.6 us -> 12.2 us  [shards(): pl.pallas_call(functools.partial(spectra_kernel, pairs), grid_spec=pltpu....]
where the time goes in v3:
time: 61.8 us; the launch traced here: 61.6 us
  Pallas kernels  60.9 us (99%)
  between operations  0.64 us (1%)
    pallas_call x1, Pallas kernels, shards(): pl.pallas_call(functools.partial(exchange_kernel, n, degree), out_shape=[...  32.7 us
    pallas_call x1, Pallas kernels, shards(): pl.pallas_call(functools.partial(wave_kernel, 1.0 / lat_count), grid=(gro...  16 us
    pallas_call x1, Pallas kernels, shards(): pl.pallas_call(functools.partial(spectra_kernel, pairs), grid_spec=pltpu....  12.2 us

profile of v3, /device:TPU:15, one launch (start us, length us, event | category | flops | bytes accessed | tf_op | source)
XLA Modules:
  0.0 61.6 jit_solution(3807305431868351898)
XLA Ops:
  0.6 12.2 %shard_map.59 = (bf16[16,32,8,128]{3,2,1,0:T(8,128)(2,1)}, f32[8,128]{1,0:T(8,128)}) custom-call(s32[32]{0:T(128)} %orders_ref.1, bf16[2049,2,1024]{2,1,0:T(2,128)(2,1)} %bitcast.5, bf16[2049,2,128]{2,1,0:T(2,128)(2,1)} %bitcast.6, s32[8,128]{1,0:T(8,128)} %bitcast.7), custom_call_target="tpu_custom_call" | custom-call | tf_op jit(solution)/shard_map/pallas_call | solution.py:186
  12.9 32.7 %shard_map.60 = (bf16[16,32,8,128]{3,2,1,0:T(8,128)(2,1)}, bf16[128,4096]{1,0:T(8,128)(2,1)}, f32[8,128]{1,0:T(8,128)}) custom-call(bf16[16,32,8,128]{3,2,1,0:T(8,128)(2,1)} %get-tuple-element.9.send_ref, f32[8,128]{1,0:T(8,128)} %get-tuple-element.10.energy_ref, s32[1,32]{1,0:T(1,128)} %bitcast.8), custom_call_target="tpu_custom_call" | custom-call | tf_op jit(solution)/shard_map/pallas_call | solution.py:213
  45.5 16.0 %shard_map.61 = (bf16[64,64,4096]{2,1,0:T(8,128)(2,1)}, f32[1,64]{1,0:T(1,128)}) custom-call(bf16[16,32,8,128]{3,2,1,0:T(8,128)(2,1)} %get-tuple-element.11.recv_ref, bf16[128,4096]{1,0:T(8,128)(2,1)} %get-tuple-element.12.basis_ref, f32[8,128]{1,0:T(8,128)} %get-tuple-element.13.total_ref), custom_call_target="tpu_custom_call" | custom-call | tf_op jit(solution)/shard_map/pallas_call | solution.py:241

commit v4 on v3

--- a/solution.py
+++ b/solution.py
@@ -103,12 +103,19 @@
             src_ref=energy_ref, dst_ref=energies.at[s], send_sem=esend_sem.at[s], recv_sem=erecv_sem.at[s],
             device_id={"blk": peer}, device_id_type=MESH)
 
-    def start(s, carry):
+    def start(i, carry):
+        s = i + 1
+        if n % 2 == 0:
+            s = n // 2 + (i % 2) * ((i + 1) // 2) - (1 - i % 2) * (i // 2)
+        block_copy(s).start()
+        return carry
+
+    def start_energy(s, carry):
         energy_copy(s).start()
-        block_copy(s).start()
-        return carry
-
-    lax.fori_loop(1, n, start, 0)
+        return carry
+
+    lax.fori_loop(0, n - 1, start, 0)
+    lax.fori_loop(1, n, start_energy, 0)
     own = pltpu.make_async_copy(send_ref.at[me], recv_ref.at[me], own_sem)
     own.start()
 

time: 61.8 us -> 63.3 us (1.024)
  the two profiles are of different devices: /device:TPU:15 before, /device:TPU:0 now
where the time goes in v4:
time: 63.3 us; the launch traced here: 63 us
  Pallas kernels  62.4 us (99%)
  between operations  0.64 us (1%)
    pallas_call x1, Pallas kernels, shards(): pl.pallas_call(functools.partial(exchange_kernel, n, degree), out_shape=[...  34.1 us
    pallas_call x1, Pallas kernels, shards(): pl.pallas_call(functools.partial(wave_kernel, 1.0 / lat_count), grid=(gro...  16 us
    pallas_call x1, Pallas kernels, shards(): pl.pallas_call(functools.partial(spectra_kernel, pairs), grid_spec=pltpu....  12.2 us

profile of v4, /device:TPU:0, one launch (start us, length us, event | category | flops | bytes accessed | tf_op | source)
XLA Modules:
  0.0 63.0 jit_solution(12784091071883788235)
XLA Ops:
  0.6 12.2 %shard_map.59 = (bf16[16,32,8,128]{3,2,1,0:T(8,128)(2,1)}, f32[8,128]{1,0:T(8,128)}) custom-call(s32[32]{0:T(128)} %orders_ref.1, bf16[2049,2,1024]{2,1,0:T(2,128)(2,1)} %bitcast.5, bf16[2049,2,128]{2,1,0:T(2,128)(2,1)} %bitcast.6, s32[8,128]{1,0:T(8,128)} %bitcast.7), custom_call_target="tpu_custom_call" | custom-call | tf_op jit(solution)/shard_map/pallas_call | solution.py:193
  12.9 34.1 %shard_map.60 = (bf16[16,32,8,128]{3,2,1,0:T(8,128)(2,1)}, bf16[128,4096]{1,0:T(8,128)(2,1)}, f32[8,128]{1,0:T(8,128)}) custom-call(bf16[16,32,8,128]{3,2,1,0:T(8,128)(2,1)} %get-tuple-element.9.send_ref, f32[8,128]{1,0:T(8,128)} %get-tuple-element.10.energy_ref, s32[1,32]{1,0:T(1,128)} %bitcast.8), custom_call_target="tpu_custom_call" | custom-call | tf_op jit(solution)/shard_map/pallas_call | solution.py:220
  47.0 16.0 %shard_map.61 = (bf16[64,64,4096]{2,1,0:T(8,128)(2,1)}, f32[1,64]{1,0:T(1,128)}) custom-call(bf16[16,32,8,128]{3,2,1,0:T(8,128)(2,1)} %get-tuple-element.11.recv_ref, bf16[128,4096]{1,0:T(8,128)(2,1)} %get-tuple-element.12.basis_ref, f32[8,128]{1,0:T(8,128)} %get-tuple-element.13.total_ref), custom_call_target="tpu_custom_call" | custom-call | tf_op jit(solution)/shard_map/pallas_call | solution.py:248
